TPU v7x, 256 devices: a whole 4x4x8 slice. The times are simulated.
256 devices in a mesh: dp: 16 (over y, x), tensor: 16 (over z, core).
Axes of the slice: x: 4, y: 4, z: 8, core: 2. Of those that a mesh axis runs over, the one named last changes fastest.
Arguments:
- tokens: bfloat16 [4096, 2048], P('dp'), may hold values from -6 to 6
- gate_weight: bfloat16 [8, 2048, 2816], P(None, 'dp', 'tensor'), may hold values from -0.25 to 0.25
- up_weight: bfloat16 [8, 2048, 2816], P(None, 'dp', 'tensor'), may hold values from -0.25 to 0.25
- down_weight: bfloat16 [8, 2816, 2048], P(None, 'tensor', 'dp'), may hold values from -0.3125 to 0.3125
- router_weight: float32 [2048, 8], replicated, may hold values from -6 to 6
- carry_mean: float32 [2048], replicated, may hold values from -0.375 to 0.375
Outputs:
- mixed: bfloat16 [4096, 2048], P(('dp', 'tensor'))
All inputs are finite; a program needn't handle non-finite values.
Results may differ from a plain program's by a relative error of at most 0.028.
Values may be sent and summed in bfloat16 or wider, within the bound.
A program may use at most 64 MiB of HBM per device.

v0:
```python
import jax
import jax.numpy as jnp
from jax import lax
from jax.sharding import PartitionSpec as P

SEG = 256
soft_cap = 8.0


def copy_for_each(array, axis):
    size = lax.axis_size(axis)
    return lax.all_to_all(
        jnp.broadcast_to(array[None], (size, *array.shape)), axis, 0, 0, tiled=True
    )


def joined_along(blocks, dim):
    blocks = jnp.moveaxis(blocks, 0, dim)
    lengths = blocks.shape
    return blocks.reshape(*lengths[:dim], lengths[dim] * lengths[dim + 1], *lengths[dim + 2 :])


def gather_directly(array, axis, dim):
    blocks = copy_for_each(array, axis)
    return joined_along(blocks, dim)


def split_up(array, dim, size):
    before, after = (array.shape[:dim], array.shape[dim + 1 :])
    return jnp.moveaxis(array.reshape(*before, size, -1, *after), dim, 0)


def sent_and_summed(array, axis, dim):
    size = lax.axis_size(axis)
    blocks = lax.all_to_all(split_up(array, dim, size), axis, 0, 0, tiled=True)
    return jnp.sum(blocks.astype(jnp.float32), axis=0)


def on_device(tokens, gate_weight, up_weight, down_weight, router_weight, carry_mean):
    dp_count = lax.axis_size("dp")
    tensor_count = lax.axis_size("tensor")
    own_rows, model_width = tokens.shape
    own_segs = own_rows // SEG
    all_segs = own_segs * dp_count
    experts, slice_rows, hidden_cols = gate_weight.shape
    own_means = jnp.sum(tokens.reshape(own_segs, SEG, model_width), axis=1, dtype=jnp.float32) / SEG
    own_logits = jnp.dot(
        own_means,
        router_weight,
        precision=lax.Precision.HIGHEST,
        preferred_element_type=jnp.float32,
    )
    seg_logits = gather_directly(own_logits, "dp", 0)
    carry_logits = jnp.dot(
        carry_mean[None, :],
        router_weight,
        precision=lax.Precision.HIGHEST,
        preferred_element_type=jnp.float32,
    )
    raw_logits = jnp.concatenate([carry_logits, seg_logits[:-1]], axis=0)
    logits = soft_cap * jnp.tanh(raw_logits / soft_cap)
    scores = jnp.exp(logits)
    probs_bf = (scores / jnp.sum(scores, axis=1, keepdims=True)).astype(jnp.bfloat16)
    gate_flat = gate_weight.reshape(experts, slice_rows * hidden_cols)
    up_flat = up_weight.reshape(experts, slice_rows * hidden_cols)
    merged_gate = jnp.dot(probs_bf, gate_flat, preferred_element_type=jnp.float32).astype(
        jnp.bfloat16
    )
    merged_up = jnp.dot(probs_bf, up_flat, preferred_element_type=jnp.float32).astype(jnp.bfloat16)
    merged_both = jnp.concatenate(
        [
            merged_gate.reshape(all_segs, slice_rows, hidden_cols),
            merged_up.reshape(all_segs, slice_rows, hidden_cols),
        ],
        axis=2,
    )
    full_rows = lax.all_to_all(merged_both, "dp", split_axis=0, concat_axis=1, tiled=True)
    own_tokens = tokens.reshape(own_segs, SEG, model_width)

    def add_block(block, total):
        rows_in = lax.dynamic_slice_in_dim(own_tokens, block * slice_rows, slice_rows, 2)
        weights_in = lax.dynamic_slice_in_dim(full_rows, block * slice_rows, slice_rows, 1)
        term = jnp.einsum("str,src->stc", rows_in, weights_in, preferred_element_type=jnp.float32)
        rounded = lax.optimization_barrier(term.astype(jnp.bfloat16))
        return total + rounded.astype(jnp.float32)

    start_total = jnp.zeros((own_segs, SEG, 2 * hidden_cols), jnp.float32)
    preact = lax.fori_loop(0, dp_count, add_block, start_total).reshape(own_rows, 2 * hidden_cols)
    hidden = (jax.nn.silu(preact[:, :hidden_cols]) * preact[:, hidden_cols:]).astype(jnp.bfloat16)
    down_cols = down_weight.shape[2]
    all_hidden = gather_directly(hidden, "dp", 0)
    merged_down = jnp.dot(
        probs_bf,
        down_weight.reshape(experts, hidden_cols * down_cols),
        preferred_element_type=jnp.float32,
    )
    merged_down = merged_down.astype(jnp.bfloat16).reshape(all_segs, hidden_cols, down_cols)
    partial_value = jnp.einsum(
        "stf,sfc->stc",
        all_hidden.reshape(all_segs, SEG, hidden_cols),
        merged_down,
        preferred_element_type=jnp.float32,
    )
    block_rows = own_rows // tensor_count
    partial_value = partial_value.reshape(dp_count, tensor_count, block_rows, down_cols)
    summed = sent_and_summed(partial_value.astype(jnp.bfloat16), "tensor", 1)
    moved = lax.all_to_all(
        summed.astype(jnp.bfloat16), "dp", split_axis=0, concat_axis=3, tiled=True
    )
    return moved.reshape(block_rows, dp_count * down_cols)


def solution(mesh):
    placed = (
        P("dp", None),
        P(None, "dp", "tensor"),
        P(None, "dp", "tensor"),
        P(None, "tensor", "dp"),
        P(),
        P(),
    )
    return jax.shard_map(
        on_device, mesh=mesh, in_specs=placed, out_specs=P(("dp", "tensor"), None), check_vma=False
    )
```

profile of v0, /device:TPU:1, one launch (start us, length us, event | category | flops | bytes accessed | tf_op | source)
XLA Modules:
  0.0 147.6 jit_solution(1069213658182428304)
XLA Ops:
  0.0 1.4 convert_reduce_fusion
  2.3 7.6 %all-to-all-start = ((f32[16,1,8]{2,1,0:T(1,128)}), f32[16,1,8]{2,1,0:T(1,128)S(1)}, u32[]{:S(2)}, u32[]{:S(2)}) async-start(f32[16,1,8]{2,1,0:T(1,128)} %broadcast_in_dim.7), calls=%async_computation | async-start | bytes 16384 | tf_op jit(solution)/shard_map/all_to_all | solution.py:12
  10.8 1.2 copy.21
  13.7 2.6 %all-to-all-done = f32[16,1,8]{2,1,0:T(1,128)S(1)} async-done(((f32[16,1,8]{2,1,0:T(1,128)}), f32[16,1,8]{2,1,0:T(1,128)S(1)}, u32[]{:S(2)}, u32[]{:S(2)}) %all-to-all-start) | async-done | bytes 544 | tf_op jit(solution)/shard_map/all_to_all | solution.py:12
  17.0 2.0 %reshape.81 = bf16[16,128,176]{2,1,0:T(8,128)(2,1)S(1)} reshape(bf16[16,22528]{1,0:T(8,128)(2,1)S(1)} %convolution_convert_fusion.3) | data formatting | bytes 1441792 | tf_op jit(solution)/shard_map/reshape | solution.py:72
  19.4 3.0 %reshape.83 = bf16[16,128,176]{2,1,0:T(8,128)(2,1)} reshape(bf16[16,22528]{1,0:T(8,128)(2,1)S(1)} %convolution_convert_fusion.2) | data formatting | bytes 1441792 | tf_op jit(solution)/shard_map/reshape | solution.py:73
  22.4 1.8 %pad_maximum_fusion = bf16[16,128,352]{2,1,0:T(8,128)(2,1)S(1)} fusion(bf16[16,128,176]{2,1,0:T(8,128)(2,1)} %reshape.83, bf16[16,128,176]{2,1,0:T(8,128)(2,1)S(1)} %reshape.81), kind=kLoop, calls=%fused_computation.12 | loop fusion | flops 2883584 | bytes 2883584 | tf_op jit(solution)/shard_map/concatenate | solution.py:70
  24.2 1.6 %copy.23 = bf16[16,128,352]{1,2,0:T(8,128)(2,1)} copy(bf16[16,128,352]{2,1,0:T(8,128)(2,1)S(1)} %pad_maximum_fusion) | data formatting | bytes 2883584 | tf_op jit(solution)/shard_map/concatenate | solution.py:70
  25.9 4.1 %all-to-all-start.1 = ((bf16[16,128,352]{1,2,0:T(8,128)(2,1)}), bf16[16,128,352]{1,2,0:T(8,128)(2,1)S(1)}, u32[]{:S(2)}, u32[]{:S(2)}) async-start(bf16[16,128,352]{1,2,0:T(8,128)(2,1)} %copy.23), calls=%async_computation.1 | async-start | bytes 2883584 | tf_op jit(solution)/shard_map/all_to_all | solution.py:77
  30.0 19.5 %all-to-all-done.1 = bf16[16,128,352]{1,2,0:T(8,128)(2,1)S(1)} async-done(((bf16[16,128,352]{1,2,0:T(8,128)(2,1)}), bf16[16,128,352]{1,2,0:T(8,128)(2,1)S(1)}, u32[]{:S(2)}, u32[]{:S(2)}) %all-to-all-start.1) | async-done | bytes 1441824 | tf_op jit(solution)/shard_map/all_to_all | solution.py:77
  50.3 19.8 %while.14 = (s32[]{:T(128)}, f32[1,256,352]{1,2,0:T(8,128)S(1)}, bf16[1,256,2048]{2,1,0:T(8,128)(2,1)}, bf16[1,2048,352]{2,1,0:T(8,128)(2,1)S(1)}, s32[]{:T(128)}, /*index=5*/s32[]{:T(128)}, s32[]{:T(128)}, s32[]{:T(128)}) while((s32[]{:T(128)}, f32[1,256,352]{1,2,0:T(8,128)S(1)}, bf16[1,256,2048]{2,1,0:T(8,128)(2,1)}, ...), condition=%wide.region_3.0_spmd.clone, body=%wide.region_2.0_spmd.clone.sunk | while | flops 23429124 | bytes 1246349 | solution.py:88
  50.3 1.1 fusion.31
  51.6 1.1 fusion.31
  55.3 1.1 fusion.31
  56.5 1.1 fusion.31
  57.8 1.1 fusion.31
  60.3 1.1 fusion.31
  62.8 1.1 fusion.31
  66.5 1.1 fusion.31
  70.3 1.2 broadcast_in_dim.8
  71.5 5.5 %all-to-all-start.2 = ((bf16[16,256,176]{1,2,0:T(8,128)(2,1)}), bf16[16,256,176]{1,2,0:T(8,128)(2,1)S(1)}, u32[]{:S(2)}, u32[]{:S(2)}) async-start(bf16[16,256,176]{1,2,0:T(8,128)(2,1)} %broadcast_in_dim.8), calls=%async_computation.2 | async-start | bytes 2883584 | tf_op jit(solution)/shard_map/all_to_all | solution.py:12
  77.5 18.8 %all-to-all-done.2 = bf16[16,256,176]{1,2,0:T(8,128)(2,1)S(1)} async-done(((bf16[16,256,176]{1,2,0:T(8,128)(2,1)}), bf16[16,256,176]{1,2,0:T(8,128)(2,1)S(1)}, u32[]{:S(2)}, u32[]{:S(2)}) %all-to-all-start.2) | async-done | bytes 1441824 | tf_op jit(solution)/shard_map/all_to_all | solution.py:12
  97.3 40.4 %all_to_all.42 = bf16[16,16,1,16,128]{4,3,1,2,0:T(8,128)(2,1)S(1)} all-to-all(bf16[16,16,1,16,128]{4,3,1,2,0:T(8,128)(2,1)S(1)} %bitcast.58), channel_id=1, replica_groups=mesh['dp'=16,'tensor'=16] {'tensor'}, dimensions={0} | all-to-all | bytes 2097152 | tf_op jit(solution)/shard_map/all_to_all | solution.py:35
  137.8 9.1 %all_to_all.43 = bf16[16,1,16,128]{3,2,1,0:T(8,128)(2,1)S(1)} all-to-all(bf16[16,1,16,128]{3,2,1,0:T(8,128)(2,1)S(1)} %bitcast.63), channel_id=1, replica_groups=mesh['dp'=16,'tensor'=16] {'dp'}, dimensions={0} | all-to-all | bytes 131072 | tf_op jit(solution)/shard_map/all_to_all | solution.py:107
  (53 shorter events, 18.1 us)
Async XLA Ops:
  0.0 1.5 copy-start
  0.0 12.8 %copy-start.1 = (bf16[8,128,176]{1,2,0:T(8,128)(2,1)S(1)}, bf16[8,128,176]{1,2,0:T(8,128)(2,1)}, u32[]{:S(2)}) copy-start(bf16[8,128,176]{1,2,0:T(8,128)(2,1)} %param.10) | copy-start | bytes 1081348
  2.3 13.9 %all-to-all-start = ((f32[16,1,8]{2,1,0:T(1,128)}), f32[16,1,8]{2,1,0:T(1,128)S(1)}, u32[]{:S(2)}, u32[]{:S(2)}) async-start(f32[16,1,8]{2,1,0:T(1,128)} %broadcast_in_dim.7), calls=%async_computation | async-start | bytes 16384 | tf_op jit(solution)/shard_map/all_to_all | solution.py:12
  25.9 23.6 %all-to-all-start.1 = ((bf16[16,128,352]{1,2,0:T(8,128)(2,1)}), bf16[16,128,352]{1,2,0:T(8,128)(2,1)S(1)}, u32[]{:S(2)}, u32[]{:S(2)}) async-start(bf16[16,128,352]{1,2,0:T(8,128)(2,1)} %copy.23), calls=%async_computation.1 | async-start | bytes 2883584 | tf_op jit(solution)/shard_map/all_to_all | solution.py:77
  71.5 5.5 %copy-start.2 = (bf16[8,176,128]{2,1,0:T(8,128)(2,1)S(1)}, bf16[8,176,128]{2,1,0:T(8,128)(2,1)}, u32[]{:S(2)}) copy-start(bf16[8,176,128]{2,1,0:T(8,128)(2,1)} %param.11) | copy-start | bytes 1081348
  71.5 24.7 %all-to-all-start.2 = ((bf16[16,256,176]{1,2,0:T(8,128)(2,1)}), bf16[16,256,176]{1,2,0:T(8,128)(2,1)S(1)}, u32[]{:S(2)}, u32[]{:S(2)}) async-start(bf16[16,256,176]{1,2,0:T(8,128)(2,1)} %broadcast_in_dim.8), calls=%async_computation.2 | async-start | bytes 2883584 | tf_op jit(solution)/shard_map/all_to_all | solution.py:12
where the time goes:
time: 149 us; the launch traced here: 148 us
  blocking collectives  49.5 us (33%)
  waiting for transfers between devices  40.8 us (27%)
  matrix products  20.7 us (14%)
  starting transfers between devices  17.1 us (11%)
  local copies, waits for them, and re-layouts  13.3 us (9%)
  other arithmetic  5.29 us (4%)
    all_to_all x1, blocking collectives, sent_and_summed(): blocks = lax.all_to_all(split_up(array, dim, size), axis, 0, 0, tiled=True)  40.4 us
    all_to_all x2, waiting for transfers between devices, copy_for_each(): lax.all_to_all(jnp.broadcast_to(array[None], (size, *array.shape)), axis,...  21.3 us
    all_to_all x1, waiting for transfers between devices, on_device(): lax.all_to_all(merged_both, 'dp', split_axis=0, concat_axis=1, tiled=True)  19.5 us
    dot_general x16, matrix products, add_block(): jnp.einsum('str,src->stc', rows_in, weights_in, preferred_element_type=jn...  17.6 us
    all_to_all x2, starting transfers between devices, copy_for_each(): lax.all_to_all(jnp.broadcast_to(array[None], (size, *array.shape)), axis,...  13 us
    all_to_all x1, blocking collectives, on_device(): lax.all_to_all(summed.astype(jnp.bfloat16), 'dp', split_axis=0, concat_ax...  9.07 us
    all_to_all x1, starting transfers between devices, on_device(): lax.all_to_all(merged_both, 'dp', split_axis=0, concat_axis=1, tiled=True)  4.09 us
    unnamed x12, local copies, waits for them, and re-layouts  3.14 us
  transfers between devices with their start and end apart: 3, of which 3 were waited for; matrix products, arithmetic and copies ran while one was open for 3% of the time, Pallas kernels for 0%

commit v1 on v0

--- a/solution.py
+++ b/solution.py
@@ -5,6 +5,12 @@
 
 SEG = 256
 soft_cap = 8.0
+
+
+def exchange_blocks(block, axis, split, join):
+    parts = jnp.split(block, lax.axis_size(axis), axis=split)
+    received = lax.all_to_all(jnp.stack(parts), axis, 0, 0)
+    return jnp.concatenate(received, axis=join)
 
 
 def copy_for_each(array, axis):
@@ -104,9 +110,7 @@
     block_rows = own_rows // tensor_count
     partial_value = partial_value.reshape(dp_count, tensor_count, block_rows, down_cols)
     summed = sent_and_summed(partial_value.astype(jnp.bfloat16), "tensor", 1)
-    moved = lax.all_to_all(
-        summed.astype(jnp.bfloat16), "dp", split_axis=0, concat_axis=3, tiled=True
-    )
+    moved = exchange_blocks(summed.astype(jnp.bfloat16), "dp", 0, 3)
     return moved.reshape(block_rows, dp_count * down_cols)
 
 

time: 149 us -> 149 us (level)
    unnamed x12 -> x27, local copies, waits for them, and re-layouts: 3.14 us -> 3.27 us
where the time goes in v1:
time: 149 us; the launch traced here: 148 us
  blocking collectives  49.5 us (33%)
  waiting for transfers between devices  40.8 us (27%)
  matrix products  20.7 us (14%)
  starting transfers between devices  17.1 us (11%)
  local copies, waits for them, and re-layouts  13.5 us (9%)
  other arithmetic  5.29 us (4%)
    all_to_all x1, blocking collectives, sent_and_summed(): blocks = lax.all_to_all(split_up(array, dim, size), axis, 0, 0, tiled=True)  40.4 us
    all_to_all x2, waiting for transfers between devices, copy_for_each(): lax.all_to_all(jnp.broadcast_to(array[None], (size, *array.shape)), axis,...  21.3 us
    all_to_all x1, waiting for transfers between devices, on_device(): lax.all_to_all(merged_both, 'dp', split_axis=0, concat_axis=1, tiled=True)  19.5 us
    dot_general x16, matrix products, add_block(): jnp.einsum('str,src->stc', rows_in, weights_in, preferred_element_type=jn...  17.6 us
    all_to_all x2, starting transfers between devices, copy_for_each(): lax.all_to_all(jnp.broadcast_to(array[None], (size, *array.shape)), axis,...  13 us
    all_to_all x1, blocking collectives, exchange_blocks(): received = lax.all_to_all(jnp.stack(parts), axis, 0, 0)  9.07 us
    all_to_all x1, starting transfers between devices, on_device(): lax.all_to_all(merged_both, 'dp', split_axis=0, concat_axis=1, tiled=True)  4.09 us
    unnamed x27, local copies, waits for them, and re-layouts  3.27 us
  transfers between devices with their start and end apart: 3, of which 3 were waited for; matrix products, arithmetic and copies ran while one was open for 3% of the time, Pallas kernels for 0%

profile of v1, /device:TPU:1, one launch (start us, length us, event | category | flops | bytes accessed | tf_op | source)
XLA Modules:
  0.0 147.8 jit_solution(15012829841106230794)
XLA Ops:
  0.0 1.4 convert_reduce_fusion
  2.3 7.6 %all-to-all-start = ((f32[16,1,8]{2,1,0:T(1,128)}), f32[16,1,8]{2,1,0:T(1,128)S(1)}, u32[]{:S(2)}, u32[]{:S(2)}) async-start(f32[16,1,8]{2,1,0:T(1,128)} %broadcast_in_dim.7), calls=%async_computation | async-start | bytes 16384 | tf_op jit(solution)/shard_map/all_to_all | solution.py:18
  10.8 1.2 copy.39
  13.7 2.6 %all-to-all-done = f32[16,1,8]{2,1,0:T(1,128)S(1)} async-done(((f32[16,1,8]{2,1,0:T(1,128)}), f32[16,1,8]{2,1,0:T(1,128)S(1)}, u32[]{:S(2)}, u32[]{:S(2)}) %all-to-all-start) | async-done | bytes 544 | tf_op jit(solution)/shard_map/all_to_all | solution.py:18
  17.0 2.0 %reshape.112 = bf16[16,128,176]{2,1,0:T(8,128)(2,1)S(1)} reshape(bf16[16,22528]{1,0:T(8,128)(2,1)S(1)} %convolution_convert_fusion.3) | data formatting | bytes 1441792 | tf_op jit(solution)/shard_map/reshape | solution.py:78
  19.4 3.0 %reshape.114 = bf16[16,128,176]{2,1,0:T(8,128)(2,1)} reshape(bf16[16,22528]{1,0:T(8,128)(2,1)S(1)} %convolution_convert_fusion.2) | data formatting | bytes 1441792 | tf_op jit(solution)/shard_map/reshape | solution.py:79
  22.4 1.8 %pad_maximum_fusion = bf16[16,128,352]{2,1,0:T(8,128)(2,1)S(1)} fusion(bf16[16,128,176]{2,1,0:T(8,128)(2,1)} %reshape.114, bf16[16,128,176]{2,1,0:T(8,128)(2,1)S(1)} %reshape.112), kind=kLoop, calls=%fused_computation.12 | loop fusion | flops 2883584 | bytes 2883584 | tf_op jit(solution)/shard_map/concatenate | solution.py:76
  24.2 1.6 %copy.41 = bf16[16,128,352]{1,2,0:T(8,128)(2,1)} copy(bf16[16,128,352]{2,1,0:T(8,128)(2,1)S(1)} %pad_maximum_fusion) | data formatting | bytes 2883584 | tf_op jit(solution)/shard_map/concatenate | solution.py:76
  25.9 4.1 %all-to-all-start.1 = ((bf16[16,128,352]{1,2,0:T(8,128)(2,1)}), bf16[16,128,352]{1,2,0:T(8,128)(2,1)S(1)}, u32[]{:S(2)}, u32[]{:S(2)}) async-start(bf16[16,128,352]{1,2,0:T(8,128)(2,1)} %copy.41), calls=%async_computation.1 | async-start | bytes 2883584 | tf_op jit(solution)/shard_map/all_to_all | solution.py:83
  30.0 19.5 %all-to-all-done.1 = bf16[16,128,352]{1,2,0:T(8,128)(2,1)S(1)} async-done(((bf16[16,128,352]{1,2,0:T(8,128)(2,1)}), bf16[16,128,352]{1,2,0:T(8,128)(2,1)S(1)}, u32[]{:S(2)}, u32[]{:S(2)}) %all-to-all-start.1) | async-done | bytes 1441824 | tf_op jit(solution)/shard_map/all_to_all | solution.py:83
  50.3 19.8 %while.14 = (s32[]{:T(128)}, f32[1,256,352]{1,2,0:T(8,128)S(1)}, bf16[1,256,2048]{2,1,0:T(8,128)(2,1)}, bf16[1,2048,352]{2,1,0:T(8,128)(2,1)S(1)}, s32[]{:T(128)}, /*index=5*/s32[]{:T(128)}, s32[]{:T(128)}, s32[]{:T(128)}) while((s32[]{:T(128)}, f32[1,256,352]{1,2,0:T(8,128)S(1)}, bf16[1,256,2048]{2,1,0:T(8,128)(2,1)}, ...), condition=%wide.region_3.0_spmd.clone, body=%wide.region_2.0_spmd.clone.sunk | while | flops 23429124 | bytes 1246349 | solution.py:94
  50.3 1.1 fusion.31
  51.6 1.1 fusion.31
  55.3 1.1 fusion.31
  56.5 1.1 fusion.31
  57.8 1.1 fusion.31
  60.3 1.1 fusion.31
  62.8 1.1 fusion.31
  66.5 1.1 fusion.31
  70.3 1.2 broadcast_in_dim.8
  71.5 5.5 %all-to-all-start.2 = ((bf16[16,256,176]{1,2,0:T(8,128)(2,1)}), bf16[16,256,176]{1,2,0:T(8,128)(2,1)S(1)}, u32[]{:S(2)}, u32[]{:S(2)}) async-start(bf16[16,256,176]{1,2,0:T(8,128)(2,1)} %broadcast_in_dim.8), calls=%async_computation.2 | async-start | bytes 2883584 | tf_op jit(solution)/shard_map/all_to_all | solution.py:18
  77.5 18.8 %all-to-all-done.2 = bf16[16,256,176]{1,2,0:T(8,128)(2,1)S(1)} async-done(((bf16[16,256,176]{1,2,0:T(8,128)(2,1)}), bf16[16,256,176]{1,2,0:T(8,128)(2,1)S(1)}, u32[]{:S(2)}, u32[]{:S(2)}) %all-to-all-start.2) | async-done | bytes 1441824 | tf_op jit(solution)/shard_map/all_to_all | solution.py:18
  97.3 40.4 %all_to_all.32 = bf16[16,16,1,16,128]{4,3,1,2,0:T(8,128)(2,1)S(1)} all-to-all(bf16[16,16,1,16,128]{4,3,1,2,0:T(8,128)(2,1)S(1)} %bitcast.117), channel_id=1, replica_groups=mesh['dp'=16,'tensor'=16] {'tensor'}, dimensions={0} | all-to-all | bytes 2097152 | tf_op jit(solution)/shard_map/all_to_all | solution.py:41
  138.0 9.1 %all_to_all.33 = bf16[16,1,1,16,128]{4,3,2,1,0:T(8,128)(2,1)S(1)} all-to-all(bf16[16,1,1,16,128]{4,3,2,1,0:T(8,128)(2,1)S(1)} %constant_dynamic-update-slice_fusion), channel_id=1, replica_groups=mesh['dp'=16,'tensor'=16] {'dp'}, dimensions={0} | all-to-all | bytes 131072 | tf_op jit(solution)/shard_map/all_to_all | solution.py:12
  (69 shorter events, 18.3 us)
Async XLA Ops:
  0.0 1.5 copy-start
  0.0 12.8 %copy-start.1 = (bf16[8,128,176]{1,2,0:T(8,128)(2,1)S(1)}, bf16[8,128,176]{1,2,0:T(8,128)(2,1)}, u32[]{:S(2)}) copy-start(bf16[8,128,176]{1,2,0:T(8,128)(2,1)} %param.10) | copy-start | bytes 1081348
  2.3 13.9 %all-to-all-start = ((f32[16,1,8]{2,1,0:T(1,128)}), f32[16,1,8]{2,1,0:T(1,128)S(1)}, u32[]{:S(2)}, u32[]{:S(2)}) async-start(f32[16,1,8]{2,1,0:T(1,128)} %broadcast_in_dim.7), calls=%async_computation | async-start | bytes 16384 | tf_op jit(solution)/shard_map/all_to_all | solution.py:18
  25.9 23.6 %all-to-all-start.1 = ((bf16[16,128,352]{1,2,0:T(8,128)(2,1)}), bf16[16,128,352]{1,2,0:T(8,128)(2,1)S(1)}, u32[]{:S(2)}, u32[]{:S(2)}) async-start(bf16[16,128,352]{1,2,0:T(8,128)(2,1)} %copy.41), calls=%async_computation.1 | async-start | bytes 2883584 | tf_op jit(solution)/shard_map/all_to_all | solution.py:83
  71.5 5.5 %copy-start.2 = (bf16[8,176,128]{2,1,0:T(8,128)(2,1)S(1)}, bf16[8,176,128]{2,1,0:T(8,128)(2,1)}, u32[]{:S(2)}) copy-start(bf16[8,176,128]{2,1,0:T(8,128)(2,1)} %param.11) | copy-start | bytes 1081348
  71.5 24.7 %all-to-all-start.2 = ((bf16[16,256,176]{1,2,0:T(8,128)(2,1)}), bf16[16,256,176]{1,2,0:T(8,128)(2,1)S(1)}, u32[]{:S(2)}, u32[]{:S(2)}) async-start(bf16[16,256,176]{1,2,0:T(8,128)(2,1)} %broadcast_in_dim.8), calls=%async_computation.2 | async-start | bytes 2883584 | tf_op jit(solution)/shard_map/all_to_all | solution.py:18
